TPU v7x, 32 devices: a whole 2x2x4 slice. The times are simulated.
32 devices in a mesh: tm: 4 (over x, core), space: 8 (over z, y).
Axes of the slice: x: 2, y: 2, z: 4, core: 2. Of those that a mesh axis runs over, the one named last changes fastest.
Arguments:
- initial_state: float32 [512, 3, 512], P('space'), may hold values from -1 to 1, as said below
- applied_field: float32 [512, 3, 512], P('space'), may hold values from -2 to 2
- coupling: float32 [512, 512], P('space'), may hold values from 0.5 to 2
Outputs:
- slice_states: float32 [4, 512, 3, 512], P('tm', 'space')
Inputs may be any that keep to these rules, and one draw needn't show every extreme that they name: `initial_state`: every cell's three components form a vector of length one.
All inputs are finite; a program needn't handle non-finite values.
Results may differ from a plain program's by a relative error of at most 0.00014.
Values sent between devices are 32-bit elements; how exact they have to be, the bound alone decides.
A program may use at most 128 MiB of HBM per device.

v0:
```python
import math

import jax
import jax.numpy as jnp
import numpy as np
from jax import lax
from jax.experimental import pallas as pl
from jax.experimental.pallas import tpu as pltpu
from jax.sharding import Mesh, PartitionSpec as P

FINE = 2
step_time = 0.06
damping = 0.02
stiffness = 0.25
thickness = 8.0

RING = ("core", "rest")
LOCAL = ("core", "zh", "rest")
EVERY = ("x", "core", "zh", "rest")


def real_tables(grid, parts):
    length = 2 * grid
    place = np.arange(grid)
    wave = np.arange(grid)
    angle = 2.0 * np.pi / length * ((place[:, None] * wave[None, :]) % length)
    cosine, sine = np.cos(angle), np.sin(angle)
    sine[:, 0] = 1.0 - 2.0 * (place % 2)
    width = grid // parts
    tall = np.concatenate([cosine, sine], axis=1).astype(np.float32)
    blocks = np.stack([cosine.reshape(grid, parts, width), sine.reshape(grid, parts, width)], axis=2)
    return tall, blocks.reshape(grid, length).astype(np.float32)


def spectral_tensor(rows, columns, length):
    wave_rows = 2.0 * math.pi / length * rows.astype(jnp.float32)
    wave_columns = 2.0 * math.pi / length * columns.astype(jnp.float32)
    squared = wave_rows * wave_rows + wave_columns * wave_columns
    nonzero = squared > 0.0
    safe = jnp.where(nonzero, squared, 1.0)
    scaled = jnp.sqrt(safe) * thickness
    film = jnp.where(nonzero, (1.0 - jnp.exp(-scaled)) / scaled, 1.0)
    in_plane = (1.0 - film) / safe
    half = length // 2
    edge_row = (rows == 0) | (rows == half)
    edge_column = (columns == 0) | (columns == half)
    weight = jnp.where(edge_row, 1.0, 2.0) * jnp.where(edge_column, 1.0, 2.0) * (-1.0 / (length * length))
    return (
        in_plane * wave_columns * wave_columns * weight,
        in_plane * wave_rows * wave_rows * weight,
        jnp.where(edge_row | edge_column, 0.0, in_plane * wave_columns * wave_rows * weight),
        film * weight,
    )


def exchange_field(padded, pad_coupling):
    center = padded[:, 1:-1]
    coupling = pad_coupling[1:-1]
    wide = jnp.pad(padded[:, 1:-1], ((0, 0), (0, 0), (1, 1)))
    wide_coupling = jnp.pad(coupling, ((0, 0), (1, 1)))
    total = pad_coupling[2:] * (padded[:, 2:] - center)
    total = total + pad_coupling[:-2] * (padded[:, :-2] - center)
    total = total + wide_coupling[:, 2:] * (wide[:, :, 2:] - center)
    total = total + wide_coupling[:, :-2] * (wide[:, :, :-2] - center)
    return stiffness * coupling * total


def cross(a, b):
    return jnp.stack([a[1] * b[2] - a[2] * b[1], a[2] * b[0] - a[0] * b[2], a[0] * b[1] - a[1] * b[0]])


def torque(magnet, effective):
    first = cross(magnet, effective)
    return -(first + damping * cross(magnet, first)) * (1.0 / (1.0 + damping * damping))


def coarse(padded, pad_coupling, field):
    center = padded[:, 1:-1]
    effective = exchange_field(padded, pad_coupling) + field
    effective = jnp.stack([effective[0], effective[1], effective[2] - center[2]])
    return center + FINE * step_time * torque(center, effective)


def dot(left, right):
    return jnp.dot(left, right, precision=lax.Precision.HIGH)


def halves(table):
    high = table.astype(jnp.bfloat16)
    return [high, (table - high.astype(np.float32)).astype(jnp.bfloat16)]


def split(value):
    high = value.astype(jnp.bfloat16)
    return high, (value - high.astype(jnp.float32)).astype(jnp.bfloat16)


def dot3(left_high, left_low, right_high, right_low):
    def one(a, b):
        return jnp.dot(a, b, preferred_element_type=jnp.float32)

    return one(left_high, right_high) + (one(left_high, right_low) + one(left_low, right_high))


def fine_kernel(
    space,
    start, field, links, coarse_end, tensors,
    cut_high, cut_low, up_high, up_low, tall_high, tall_low, back_high, back_low,
    out,
    current, rate, base, edge_out, edge_in, send, got, send_back, got_back,
    columns_high, columns_low, mixed_high, mixed_low, wide_high, wide_low, demag,
    edge_sems, send_sems, got_sems, send_back_sems, got_back_sems,
):
    _, rows, grid = start.shape
    rest = space // 2
    width = 2 * grid // space
    part = lax.axis_index("core") * rest + lax.axis_index("rest")

    def device(target):
        return {"core": target // rest, "rest": target % rest}

    barrier = pltpu.get_barrier_semaphore()

    def greet(k, carry):
        pl.semaphore_signal(
            barrier, inc=1, device_id=device((part + k) % space), device_id_type=pl.DeviceIdType.MESH
        )
        return carry

    lax.fori_loop(1, space, greet, 0)
    pl.semaphore_wait(barrier, space - 1)

    def remote(source, target, send_sem, recv_sem, where):
        return pltpu.make_async_remote_copy(
            src_ref=source, dst_ref=target, send_sem=send_sem, recv_sem=recv_sem,
            device_id=device(where), device_id_type=pl.DeviceIdType.MESH,
        )

    def forward(k):
        target = (part + k) % space
        return remote(send.at[target], got.at[part], send_sems.at[k], got_sems.at[k], target)

    def backward(k):
        target = (part + k) % space
        return remote(
            send_back.at[target], got_back.at[part], send_back_sems.at[k], got_back_sems.at[k], target
        )

    current[:, 8 : 8 + rows, :] = start[...]
    base[...] = start[...]

    def evaluate(parity):
        for c in range(3):
            edge_out[0, c : c + 1, :] = current[c, 8:9, :]
            edge_out[1, c : c + 1, :] = current[c, 7 + rows : 8 + rows, :]
        magnet_high, magnet_low = split(current[:, 8 : 8 + rows, :].reshape(3 * rows, grid))
        wide_high[:, :grid] = magnet_high
        wide_low[:, :grid] = magnet_low

        def block(index):
            return dot3(wide_high[:, :grid], wide_low[:, :grid], cut_high[index], cut_low[index])

        to_before = remote(
            edge_out.at[0], edge_in.at[parity, 1], edge_sems.at[0], edge_sems.at[1], (part + space - 1) % space
        )
        to_after = remote(
            edge_out.at[1], edge_in.at[parity, 0], edge_sems.at[2], edge_sems.at[3], (part + 1) % space
        )
        to_before.start()
        to_after.start()

        def push(k, carry):
            target = (part + k) % space
            send[target] = block(target)
            forward(k).start()
            return carry

        lax.fori_loop(1, space, push, 0)
        got[part] = block(part)

        def take(k, carry):
            forward(k).wait()
            return carry

        lax.fori_loop(1, space, take, 0)
        to_before.wait()
        to_after.wait()
        for c in range(3):
            current[c, 7:8, :] = edge_in[parity, 0, c : c + 1, :]
            current[c, 8 + rows : 9 + rows, :] = edge_in[parity, 1, c : c + 1, :]
        columns = jnp.concatenate(
            [got[:, c * rows : (c + 1) * rows, :].reshape(grid, width) for c in range(3)], axis=1
        )
        columns_high[...], columns_low[...] = split(columns)

        step = grid // 2

        def mix(i, carry):
            lower = pl.multiple_of(i * step, step)
            upper = pl.multiple_of(grid + i * step, step)

            def spectrum(at):
                return dot3(
                    up_high[pl.ds(at, step), :], up_low[pl.ds(at, step), :], columns_high[...], columns_low[...]
                )

            pair = (spectrum(lower), spectrum(upper))
            for q, at in enumerate((lower, upper)):
                txx, tyy, txy, tzz = (tensors[n, pl.ds(at, step), :] for n in range(4))
                sx, sy, sz = (pair[q][:, c * width : (c + 1) * width] for c in range(3))
                ox, oy = (pltpu.roll(pair[1 - q][:, c * width : (c + 1) * width], width // 2, 1) for c in range(2))
                for c, value in enumerate((txx * sx + txy * oy, txy * ox + tyy * sy, tzz * sz)):
                    high, low = split(value)
                    mixed_high[pl.ds(at, step), c * width : (c + 1) * width] = high
                    mixed_low[pl.ds(at, step), c * width : (c + 1) * width] = low
            return carry

        lax.fori_loop(0, 2, mix, 0)

        def synth(i, carry):
            at = pl.multiple_of(i * step, step)
            value = dot3(
                tall_high[pl.ds(at, step), :], tall_low[pl.ds(at, step), :], mixed_high[...], mixed_low[...]
            )
            send_back[pl.ds(i * (space // 2), space // 2)] = value.reshape(space // 2, rows, 3 * width)
            return carry

        lax.fori_loop(0, 2, synth, 0)

        def push_back(k, carry):
            backward(k).start()
            return carry

        lax.fori_loop(1, space, push_back, 0)
        got_back[part] = send_back[part]

        def take_back(k, carry):
            backward(k).wait()
            return carry

        lax.fori_loop(1, space, take_back, 0)
        for j in range(space):
            for c in range(3):
                high, low = split(got_back[j, :, c * width : (c + 1) * width])
                wide_high[c * rows : (c + 1) * rows, j * width : (j + 1) * width] = high
                wide_low[c * rows : (c + 1) * rows, j * width : (j + 1) * width] = low
        demag[...] = dot3(wide_high[...], wide_low[...], back_high[...], back_low[...])

        for at in range(0, rows, 8):
            inside = [current[c, 8 + at : 16 + at, :] for c in range(3)]
            weights = [links[n, at : at + 8, :] for n in range(4)]
            effective = []
            for c in range(3):
                m = inside[c]
                total = weights[0] * (current[c, 7 + at : 15 + at, :] - m)
                total = total + weights[1] * (current[c, 9 + at : 17 + at, :] - m)
                total = total + weights[2] * (pltpu.roll(m, 1, 1) - m)
                total = total + weights[3] * (pltpu.roll(m, grid - 1, 1) - m)
                effective.append(total + demag[c * rows + at : c * rows + at + 8, :] + field[c, at : at + 8, :])
            first = cross_of(inside, effective)
            second = cross_of(inside, first)
            for c in range(3):
                value = -(first[c] + damping * second[c]) * (1.0 / (1.0 + damping * damping))
                if parity == 0:
                    rate[c, at : at + 8, :] = value
                else:
                    moved = base[c, at : at + 8, :] + 0.5 * step_time * (rate[c, at : at + 8, :] + value)
                    base[c, at : at + 8, :] = moved
        if parity == 0:
            current[:, 8 : 8 + rows, :] = base[...] + step_time * rate[...]
        else:
            current[:, 8 : 8 + rows, :] = base[...]

    def fine_step(i, carry):
        evaluate(0)
        evaluate(1)
        return carry

    lax.fori_loop(0, FINE, fine_step, 0)
    out[...] = base[...] - coarse_end[...]


def cross_of(a, b):
    return [a[1] * b[2] - a[2] * b[1], a[2] * b[0] - a[0] * b[2], a[0] * b[1] - a[1] * b[0]]


def fine_jump(space, start, field, links, coarse_end, tensors, tables):
    _, rows, grid = start.shape
    length = 2 * grid
    width = length // space

    def kernel(*refs):
        fine_kernel(space, *refs)

    f32, bf16 = jnp.float32, jnp.bfloat16
    operands = [start, field, links, coarse_end, tensors, *tables]
    return pl.pallas_call(
        kernel,
        out_shape=jax.ShapeDtypeStruct(start.shape, f32),
        in_specs=[pl.BlockSpec(memory_space=pltpu.VMEM)] * len(operands),
        out_specs=pl.BlockSpec(memory_space=pltpu.VMEM),
        scratch_shapes=[
            pltpu.VMEM((3, rows + 16, grid), f32),
            pltpu.VMEM((3, rows, grid), f32),
            pltpu.VMEM((3, rows, grid), f32),
            pltpu.VMEM((2, 8, grid), f32),
            pltpu.VMEM((2, 2, 8, grid), f32),
            pltpu.VMEM((space, 3 * rows, width), f32),
            pltpu.VMEM((space, 3 * rows, width), f32),
            pltpu.VMEM((space, rows, 3 * width), f32),
            pltpu.VMEM((space, rows, 3 * width), f32),
            pltpu.VMEM((grid, 3 * width), bf16),
            pltpu.VMEM((grid, 3 * width), bf16),
            pltpu.VMEM((length, 3 * width), bf16),
            pltpu.VMEM((length, 3 * width), bf16),
            pltpu.VMEM((3 * rows, length), bf16),
            pltpu.VMEM((3 * rows, length), bf16),
            pltpu.VMEM((3 * rows, grid), f32),
            pltpu.SemaphoreType.DMA((4,)),
            pltpu.SemaphoreType.DMA((space,)),
            pltpu.SemaphoreType.DMA((space,)),
            pltpu.SemaphoreType.DMA((space,)),
            pltpu.SemaphoreType.DMA((space,)),
        ],
        compiler_params=pltpu.CompilerParams(
            collective_id=0, has_side_effects=True, vmem_limit_bytes=56 * 1024 * 1024
        ),
    )(*operands)


def make_shards(tm, space):
    rest = space // 2

    def swapped(role):
        core, zh, r = role // space, role // rest % 2, role % rest
        return zh * space + core * rest + r

    def shards(initial_state, applied_field, coupling):
        rows, _, grid = initial_state.shape
        length = 2 * grid
        width = length // space
        depth = tm
        part = lax.axis_index(RING)
        old_slice = lax.axis_index(("x", "core"))
        new_slice = lax.axis_index(("x", "zh"))
        tall, blocks = real_tables(grid, space)

        start = jnp.transpose(initial_state, (1, 0, 2))
        field = jnp.transpose(applied_field, (1, 0, 2))
        pack = jnp.concatenate([start, field, coupling[None]], axis=0)

        def fetch(block, shift):
            pairs = []
            for device in range(2 * space):
                core, zh, r = device // space, device // rest % 2, device % rest
                wanted = core * rest + r + shift
                if 0 <= wanted < space:
                    pairs.append((zh * space + wanted, device))
            return lax.ppermute(block, LOCAL, pairs)

        middle = fetch(pack, 0)
        before = fetch(pack[:, rows - depth :], -1)
        after = fetch(pack[:, :depth], 1)
        wide = jnp.concatenate([before, middle, after], axis=1)
        wide_coupling = wide[6]
        wide_field = wide[3:6]
        state = wide[:3]
        fine_start, coarse_end = state, state
        for n in range(tm):
            stepped = jnp.pad(
                coarse(state, wide_coupling, wide_field[:, 1:-1]), ((0, 0), (1, 1), (0, 0))
            )
            here = new_slice == n
            fine_start = jnp.where(here, state, fine_start)
            coarse_end = jnp.where(here, stepped, coarse_end)
            state = stepped
        fine_field = wide_field[:, depth:-depth]
        fine_coupling = wide_coupling[depth - 1 : rows + depth + 1]
        coarse_end = coarse_end[:, depth:-depth]

        slot = jnp.arange(length, dtype=jnp.int32)
        wave_y = jnp.where(slot == grid, grid, slot % grid)
        lane = jnp.arange(width, dtype=jnp.int32)
        wave_x = part * (width // 2) + lane % (width // 2)
        wave_x = jnp.where((wave_x == 0) & (lane >= width // 2), grid, wave_x)
        txx, tyy, txy, tzz = spectral_tensor(wave_y[:, None], wave_x[None, :], length)
        same = ((slot >= grid)[:, None]) == ((lane >= width // 2)[None, :])
        txy = jnp.where(same, -txy, txy)

        own = wide_coupling[depth : rows + depth]
        flat = jnp.pad(own, ((0, 0), (1, 1)))
        links = stiffness * own[None] * jnp.stack(
            [
                wide_coupling[depth - 1 : rows + depth - 1],
                wide_coupling[depth + 1 : rows + depth + 1],
                flat[:, :-2],
                flat[:, 2:],
            ]
        )
        cut = np.transpose(blocks.reshape(grid, space, width), (1, 0, 2))
        tables = [part_ for table in (cut, tall.T, tall, blocks.T) for part_ in halves(table)]
        jump = fine_jump(
            space, fine_start[:, depth:-depth], fine_field, links, coarse_end, jnp.stack([txx, tyy, txy, tzz]), tables
        )
        jump = lax.ppermute(jump, LOCAL, [(swapped(i), i) for i in range(2 * space)])

        def along(block, slice_shift, row_shift):
            pairs = []
            for device in range(tm * space):
                n, s = device // space - slice_shift, device % space + row_shift
                if 0 <= n and 0 <= s < space:
                    pairs.append((n * space + s, device))
            return lax.ppermute(block, EVERY, pairs)

        def padded_from(block, slice_shift, with_middle):
            up = along(block[:, -1:], slice_shift, -1)
            down = along(block[:, :1], slice_shift, 1)
            middle = along(block[:3], slice_shift, 0) if with_middle else block
            return jnp.concatenate([up, middle, down], axis=1)

        home = padded_from(jnp.concatenate([start, coupling[None]], axis=0), 0, False)
        home_state, home_coupling = home[:3], home[3]
        end = coarse(home_state, home_coupling, field) + jump
        for n in range(1, tm):
            current = jnp.where(old_slice == 0, home_state, padded_from(end, 1, True))
            end = coarse(current, home_coupling, field) + jump
        return jnp.transpose(end, (1, 0, 2))[None]

    return shards


def solution(mesh):
    tm, space = mesh.shape["tm"], mesh.shape["space"]
    finer = Mesh(mesh.devices.reshape(tm // 2, 2, 2, space // 2), EVERY)
    rows = ("zh", "rest")
    return jax.shard_map(
        make_shards(tm, space),
        mesh=finer,
        in_specs=(P(rows, None, None), P(rows, None, None), P(rows, None)),
        out_specs=P(("x", "core"), rows, None, None),
        check_vma=False,
    )
```

profile of v0, /device:TPU:18, one launch (start us, length us, event | category | flops | bytes accessed | tf_op | source)
XLA Modules:
  0.0 201.6 jit_solution(10012328544592278427)
XLA Ops:
  0.0 1.3 pad_maximum_fusion.2
  1.3 1.9 collective-permute-start.3
  3.9 5.5 %collective-permute-start.2 = (f32[7,4,512]{2,1,0:T(4,128)}, f32[7,4,512]{2,1,0:T(4,128)S(1)}, u32[]{:S(2)}, u32[]{:S(2)}) collective-permute-start(f32[7,4,512]{2,1,0:T(4,128)} %get-tuple-element.53), channel_id=1, source_target_pairs={{0,1},{1,2},{2,3},{8,5},{9,6},{10,7},{3,8},{4,9},{5,10},{6,11},{11... | collective-permute-start | bytes 172040 | tf_op jit(solution)/shard_map/ppermute | solution.py:359
  9.4 2.4 %collective-permute-start.4 = (f32[7,4,512]{2,1,0:T(4,128)}, f32[7,4,512]{2,1,0:T(4,128)S(1)}, u32[]{:S(2)}, u32[]{:S(2)}) collective-permute-start(f32[7,4,512]{2,1,0:T(4,128)} %get-tuple-element.54), channel_id=1, source_target_pairs={{1,0},{2,1},{3,2},{4,3},{9,4},{10,5},{11,6},{12,7},{5,8},{6,9},{7,... | collective-permute-start | bytes 172040 | tf_op jit(solution)/shard_map/ppermute | solution.py:359
  11.9 2.9 %collective-permute-start = (f32[4,1,512]{2,1,0:T(1,128)S(1)}, f32[4,1,512]{2,1,0:T(1,128)S(1)}, u32[]{:S(2)}, u32[]{:S(2)}) collective-permute-start(f32[4,1,512]{2,1,0:T(1,128)S(1)} %get-tuple-element.58), channel_id=1, source_target_pairs={{0,1},{1,2},{2,3},{3,4},{4,5},{5,6},{6,7},{8,9},{9,10},{10,11},{11... | collective-permute-start | bytes 24584 | tf_op jit(solution)/shard_map/ppermute | solution.py:413
  14.8 3.9 %collective-permute-start.1 = (f32[4,1,512]{2,1,0:T(1,128)S(1)}, f32[4,1,512]{2,1,0:T(1,128)S(1)}, u32[]{:S(2)}, u32[]{:S(2)}) collective-permute-start(f32[4,1,512]{2,1,0:T(1,128)S(1)} %get-tuple-element.57), channel_id=1, source_target_pairs={{1,0},{2,1},{3,2},{4,3},{5,4},{6,5},{7,6},{9,8},{10,9},{11,10},{12... | collective-permute-start | bytes 24584 | tf_op jit(solution)/shard_map/ppermute | solution.py:413
  19.6 1.5 pad_maximum_fusion.refs_4_
  21.1 5.5 %collective-permute-done.1 = f32[4,1,512]{2,1,0:T(1,128)S(1)} collective-permute-done((f32[4,1,512]{2,1,0:T(1,128)S(1)}, f32[4,1,512]{2,1,0:T(1,128)S(1)}, u32[]{:S(2)}, u32[]{:S(2)}) %collective-permute-start.1) | collective-permute-done | bytes 8224 | tf_op jit(solution)/shard_map/ppermute | solution.py:413
  34.4 118.5 %shard_map.109 = f32[3,64,512]{2,1,0:T(8,128)} custom-call(f32[3,64,512]{2,1,0:T(8,128)} %get-tuple-element.46.refs_0_, f32[3,64,512]{2,1,0:T(8,128)} %slice.684.refs_1_, f32[4,64,512]{2,1,0:T(8,128)} %fusion.11.refs_2_, f32[3,64,512]{2,1,0:T(8,128)} %get-tuple-element.45.refs_3_, f32[4,1024,128]{2,1,0:T(8,128)} %pad_maximum_fusion.refs_4_, ...), custom_call_target="tpu_custom_call" | custom-call | tf_op jit(solution)/shard_map/pallas_call | solution.py:297
  152.9 1.9 collective-permute-start.5
  154.9 9.7 %collective-permute-done.5 = f32[3,64,512]{2,1,0:T(8,128)S(1)} collective-permute-done((f32[3,64,512]{2,1,0:T(8,128)}, f32[3,64,512]{2,1,0:T(8,128)S(1)}, u32[]{:S(2)}, u32[]{:S(2)}) %collective-permute-start.5) | collective-permute-done | bytes 393248 | tf_op jit(solution)/shard_map/ppermute | solution.py:405
  164.8 1.9 collective-permute-start.7
  166.7 1.9 collective-permute-start.6
  168.7 2.7 %collective-permute-start.8 = (f32[3,1,512]{2,1,0:T(1,128)S(1)}, f32[3,1,512]{2,1,0:T(1,128)S(1)}, u32[]{:S(2)}, u32[]{:S(2)}) collective-permute-start(f32[3,1,512]{2,1,0:T(1,128)S(1)} %get-tuple-element.64), channel_id=1, source_target_pairs={{1,8},{2,9},{3,10},{4,11},{5,12},{6,13},{7,14},{9,16},{10,17},{11,... | collective-permute-start | bytes 18440 | tf_op jit(solution)/shard_map/ppermute | solution.py:413
  171.4 2.2 %collective-permute-done.6 = f32[3,1,512]{2,1,0:T(1,128)S(1)} collective-permute-done((f32[3,1,512]{2,1,0:T(1,128)S(1)}, f32[3,1,512]{2,1,0:T(1,128)S(1)}, u32[]{:S(2)}, u32[]{:S(2)}) %collective-permute-start.6) | collective-permute-done | bytes 6176 | tf_op jit(solution)/shard_map/ppermute | solution.py:413
  173.6 3.8 %collective-permute-done.8 = f32[3,1,512]{2,1,0:T(1,128)S(1)} collective-permute-done((f32[3,1,512]{2,1,0:T(1,128)S(1)}, f32[3,1,512]{2,1,0:T(1,128)S(1)}, u32[]{:S(2)}, u32[]{:S(2)}) %collective-permute-start.8) | collective-permute-done | bytes 6176 | tf_op jit(solution)/shard_map/ppermute | solution.py:413
  178.3 1.9 collective-permute-start.10
  180.3 1.9 collective-permute-start.11
  182.2 1.9 collective-permute-start.9
  184.1 4.3 %collective-permute-done.11 = f32[3,1,512]{2,1,0:T(1,128)S(1)} collective-permute-done((f32[3,1,512]{2,1,0:T(1,128)S(1)}, f32[3,1,512]{2,1,0:T(1,128)S(1)}, u32[]{:S(2)}, u32[]{:S(2)}) %collective-permute-start.11) | collective-permute-done | bytes 6176 | tf_op jit(solution)/shard_map/ppermute | solution.py:413
  189.9 1.9 collective-permute-start.13
  191.9 1.9 collective-permute-start.12
  193.8 1.9 collective-permute-start.14
  195.7 3.0 %collective-permute-done.12 = f32[3,1,512]{2,1,0:T(1,128)S(1)} collective-permute-done((f32[3,1,512]{2,1,0:T(1,128)S(1)}, f32[3,1,512]{2,1,0:T(1,128)S(1)}, u32[]{:S(2)}, u32[]{:S(2)}) %collective-permute-start.12) | collective-permute-done | bytes 6176 | tf_op jit(solution)/shard_map/ppermute | solution.py:413
  (85 shorter events, 14.8 us)
Async XLA Ops:
  0.0 11.8 %copy-start = (f32[64,3,512]{2,0,1:T(8,128)S(1)}, f32[64,3,512]{2,0,1:T(8,128)}, u32[]{:S(2)}) copy-start(f32[64,3,512]{2,0,1:T(8,128)} %param.11) | copy-start | bytes 1179652
  0.0 11.8 %copy-start.2 = (f32[64,512]{1,0:T(8,128)S(1)}, f32[64,512]{1,0:T(8,128)}, u32[]{:S(2)}) copy-start(f32[64,512]{1,0:T(8,128)} %param.13) | copy-start | bytes 393220
  1.3 25.8 %collective-permute-start.3 = (f32[7,64,512]{2,1,0:T(8,128)S(1)}, f32[7,64,512]{2,1,0:T(8,128)S(1)}, u32[]{:S(2)}, u32[]{:S(2)}) collective-permute-start(f32[7,64,512]{2,1,0:T(8,128)S(1)} %pad_maximum_fusion.2), channel_id=1, source_target_pairs={{0,0},{1,1},{2,2},{3,3},{8,4},{9,5},{10,6},{11,7},{4,8},{5,9},{6,1... | collective-permute-start | bytes 2752520 | tf_op jit(solution)/shard_map/ppermute | solution.py:359
  3.9 23.1 %collective-permute-start.2 = (f32[7,4,512]{2,1,0:T(4,128)}, f32[7,4,512]{2,1,0:T(4,128)S(1)}, u32[]{:S(2)}, u32[]{:S(2)}) collective-permute-start(f32[7,4,512]{2,1,0:T(4,128)} %get-tuple-element.53), channel_id=1, source_target_pairs={{0,1},{1,2},{2,3},{8,5},{9,6},{10,7},{3,8},{4,9},{5,10},{6,11},{11... | collective-permute-start | bytes 172040 | tf_op jit(solution)/shard_map/ppermute | solution.py:359
  9.4 17.7 %collective-permute-start.4 = (f32[7,4,512]{2,1,0:T(4,128)}, f32[7,4,512]{2,1,0:T(4,128)S(1)}, u32[]{:S(2)}, u32[]{:S(2)}) collective-permute-start(f32[7,4,512]{2,1,0:T(4,128)} %get-tuple-element.54), channel_id=1, source_target_pairs={{1,0},{2,1},{3,2},{4,3},{9,4},{10,5},{11,6},{12,7},{5,8},{6,9},{7,... | collective-permute-start | bytes 172040 | tf_op jit(solution)/shard_map/ppermute | solution.py:359
  11.9 9.3 %collective-permute-start = (f32[4,1,512]{2,1,0:T(1,128)S(1)}, f32[4,1,512]{2,1,0:T(1,128)S(1)}, u32[]{:S(2)}, u32[]{:S(2)}) collective-permute-start(f32[4,1,512]{2,1,0:T(1,128)S(1)} %get-tuple-element.58), channel_id=1, source_target_pairs={{0,1},{1,2},{2,3},{3,4},{4,5},{5,6},{6,7},{8,9},{9,10},{10,11},{11... | collective-permute-start | bytes 24584 | tf_op jit(solution)/shard_map/ppermute | solution.py:413
  14.8 11.9 %collective-permute-start.1 = (f32[4,1,512]{2,1,0:T(1,128)S(1)}, f32[4,1,512]{2,1,0:T(1,128)S(1)}, u32[]{:S(2)}, u32[]{:S(2)}) collective-permute-start(f32[4,1,512]{2,1,0:T(1,128)S(1)} %get-tuple-element.57), channel_id=1, source_target_pairs={{1,0},{2,1},{3,2},{4,3},{5,4},{6,5},{7,6},{9,8},{10,9},{11,10},{12... | collective-permute-start | bytes 24584 | tf_op jit(solution)/shard_map/ppermute | solution.py:413
  19.6 7.0 %copy-start.1 = (f32[64,3,512]{2,0,1:T(8,128)S(1)}, f32[64,3,512]{2,0,1:T(8,128)}, u32[]{:S(2)}) copy-start(f32[64,3,512]{2,0,1:T(8,128)} %param.12) | copy-start | bytes 1179652
  152.9 11.7 %collective-permute-start.5 = (f32[3,64,512]{2,1,0:T(8,128)}, f32[3,64,512]{2,1,0:T(8,128)S(1)}, u32[]{:S(2)}, u32[]{:S(2)}) collective-permute-start(f32[3,64,512]{2,1,0:T(8,128)} %shard_map.109), channel_id=1, source_target_pairs={{0,0},{1,1},{2,2},{3,3},{8,4},{9,5},{10,6},{11,7},{4,8},{5,9},{6,1... | collective-permute-start | bytes 1179656 | tf_op jit(solution)/shard_map/ppermute | solution.py:405
  164.8 12.6 %collective-permute-start.7 = (f32[3,64,512]{2,1,0:T(8,128)S(1)}, f32[3,64,512]{2,1,0:T(8,128)S(1)}, u32[]{:S(2)}, u32[]{:S(2)}) collective-permute-start(f32[3,64,512]{2,1,0:T(8,128)S(1)} %fusion.111), channel_id=1, source_target_pairs={{0,8},{1,9},{2,10},{3,11},{4,12},{5,13},{6,14},{7,15},{8,16},{9,17... | collective-permute-start | bytes 1179656 | tf_op jit(solution)/shard_map/ppermute | solution.py:413
  166.7 6.8 %collective-permute-start.6 = (f32[3,1,512]{2,1,0:T(1,128)S(1)}, f32[3,1,512]{2,1,0:T(1,128)S(1)}, u32[]{:S(2)}, u32[]{:S(2)}) collective-permute-start(f32[3,1,512]{2,1,0:T(1,128)S(1)} %get-tuple-element.63), channel_id=1, source_target_pairs={{0,9},{1,10},{2,11},{3,12},{4,13},{5,14},{6,15},{8,17},{9,18},{10,... | collective-permute-start | bytes 18440 | tf_op jit(solution)/shard_map/ppermute | solution.py:413
  168.7 8.7 %collective-permute-start.8 = (f32[3,1,512]{2,1,0:T(1,128)S(1)}, f32[3,1,512]{2,1,0:T(1,128)S(1)}, u32[]{:S(2)}, u32[]{:S(2)}) collective-permute-start(f32[3,1,512]{2,1,0:T(1,128)S(1)} %get-tuple-element.64), channel_id=1, source_target_pairs={{1,8},{2,9},{3,10},{4,11},{5,12},{6,13},{7,14},{9,16},{10,17},{11,... | collective-permute-start | bytes 18440 | tf_op jit(solution)/shard_map/ppermute | solution.py:413
  178.3 10.6 %collective-permute-start.10 = (f32[3,64,512]{2,1,0:T(8,128)S(1)}, f32[3,64,512]{2,1,0:T(8,128)S(1)}, u32[]{:S(2)}, u32[]{:S(2)}) collective-permute-start(f32[3,64,512]{2,1,0:T(8,128)S(1)} %fusion.115), channel_id=1, source_target_pairs={{0,8},{1,9},{2,10},{3,11},{4,12},{5,13},{6,14},{7,15},{8,16},{9,17... | collective-permute-start | bytes 1179656 | tf_op jit(solution)/shard_map/ppermute | solution.py:413
  180.3 8.1 %collective-permute-start.11 = (f32[3,1,512]{2,1,0:T(1,128)S(1)}, f32[3,1,512]{2,1,0:T(1,128)S(1)}, u32[]{:S(2)}, u32[]{:S(2)}) collective-permute-start(f32[3,1,512]{2,1,0:T(1,128)S(1)} %get-tuple-element.62), channel_id=1, source_target_pairs={{1,8},{2,9},{3,10},{4,11},{5,12},{6,13},{7,14},{9,16},{10,17},{11,... | collective-permute-start | bytes 18440 | tf_op jit(solution)/shard_map/ppermute | solution.py:413
  182.2 6.7 %collective-permute-start.9 = (f32[3,1,512]{2,1,0:T(1,128)S(1)}, f32[3,1,512]{2,1,0:T(1,128)S(1)}, u32[]{:S(2)}, u32[]{:S(2)}) collective-permute-start(f32[3,1,512]{2,1,0:T(1,128)S(1)} %get-tuple-element.61), channel_id=1, source_target_pairs={{0,9},{1,10},{2,11},{3,12},{4,13},{5,14},{6,15},{8,17},{9,18},{10,... | collective-permute-start | bytes 18440 | tf_op jit(solution)/shard_map/ppermute | solution.py:413
  189.9 10.0 %collective-permute-start.13 = (f32[3,64,512]{2,1,0:T(8,128)S(1)}, f32[3,64,512]{2,1,0:T(8,128)S(1)}, u32[]{:S(2)}, u32[]{:S(2)}) collective-permute-start(f32[3,64,512]{2,1,0:T(8,128)S(1)} %fusion.119), channel_id=1, source_target_pairs={{0,8},{1,9},{2,10},{3,11},{4,12},{5,13},{6,14},{7,15},{8,16},{9,17... | collective-permute-start | bytes 1179656 | tf_op jit(solution)/shard_map/ppermute | solution.py:413
  191.9 6.8 %collective-permute-start.12 = (f32[3,1,512]{2,1,0:T(1,128)S(1)}, f32[3,1,512]{2,1,0:T(1,128)S(1)}, u32[]{:S(2)}, u32[]{:S(2)}) collective-permute-start(f32[3,1,512]{2,1,0:T(1,128)S(1)} %get-tuple-element.59), channel_id=1, source_target_pairs={{0,9},{1,10},{2,11},{3,12},{4,13},{5,14},{6,15},{8,17},{9,18},{10,... | collective-permute-start | bytes 18440 | tf_op jit(solution)/shard_map/ppermute | solution.py:413
  193.8 6.1 %collective-permute-start.14 = (f32[3,1,512]{2,1,0:T(1,128)S(1)}, f32[3,1,512]{2,1,0:T(1,128)S(1)}, u32[]{:S(2)}, u32[]{:S(2)}) collective-permute-start(f32[3,1,512]{2,1,0:T(1,128)S(1)} %get-tuple-element.60), channel_id=1, source_target_pairs={{1,8},{2,9},{3,10},{4,11},{5,12},{6,13},{7,14},{9,16},{10,17},{11,... | collective-permute-start | bytes 18440 | tf_op jit(solution)/shard_map/ppermute | solution.py:413
where the time goes:
time: 205 us; the launch traced here: 202 us
  Pallas kernels  118 us (58%)
  starting transfers between devices  36.5 us (18%)
  waiting for transfers between devices  30.2 us (15%)
  other arithmetic  13.9 us (7%)
    pallas_call x1, Pallas kernels, fine_jump(): pl.pallas_call(kernel, out_shape=jax.ShapeDtypeStruct(start.shape, f32),...  118 us
    ppermute x11, starting transfers between devices, along(): return lax.ppermute(block, EVERY, pairs)  24.8 us
    ppermute x11, waiting for transfers between devices, along(): return lax.ppermute(block, EVERY, pairs)  20.5 us
    ppermute x3, starting transfers between devices, fetch(): return lax.ppermute(block, LOCAL, pairs)  9.82 us
    ppermute x1, waiting for transfers between devices, shards(): lax.ppermute(jump, LOCAL, [(swapped(i), i) for i in range(2 * space)])  9.68 us
  transfers between devices with their start and end apart: 15, of which 8 were waited for; matrix products, arithmetic and copies ran while one was open for 2% of the time, Pallas kernels for 0%

commit v1 on v0

--- a/solution.py
+++ b/solution.py
@@ -223,15 +223,20 @@
                 tall_high[pl.ds(at, step), :], tall_low[pl.ds(at, step), :], mixed_high[...], mixed_low[...]
             )
             send_back[pl.ds(i * (space // 2), space // 2)] = value.reshape(space // 2, rows, 3 * width)
-            return carry
+
+            def push_back(j, inner):
+                target = i * (space // 2) + j
+
+                @pl.when(target != part)
+                def _():
+                    backward((target - part + space) % space).start()
+
+                return inner
+
+            return lax.fori_loop(0, space // 2, push_back, carry)
 
         lax.fori_loop(0, 2, synth, 0)
 
-        def push_back(k, carry):
-            backward(k).start()
-            return carry
-
-        lax.fori_loop(1, space, push_back, 0)
         got_back[part] = send_back[part]
 
         def take_back(k, carry):
@@ -328,12 +333,164 @@
     )(*operands)
 
 
+def links_of(pad_coupling, depth):
+    rows = pad_coupling.shape[0] - 2 * depth
+    own = pad_coupling[depth : rows + depth]
+    flat = jnp.pad(own, ((0, 0), (1, 1)))
+    around = [
+        pad_coupling[depth - 1 : rows + depth - 1],
+        pad_coupling[depth + 1 : rows + depth + 1],
+        flat[:, :-2],
+        flat[:, 2:],
+    ]
+    return stiffness * own[None] * jnp.stack(around)
+
+
+def sweep_kernel(
+    space, tm, jump, opening, field, links, out,
+    current, landed, edge_out, edge_in, swap_sems, send_sems, recv_sems,
+):
+    _, rows, grid = opening.shape
+    rest = space // 2
+    core, zh = lax.axis_index("core"), lax.axis_index("zh")
+    number = lax.axis_index("x") * 2 + core
+    place = zh * rest + lax.axis_index("rest")
+    mesh_type = pl.DeviceIdType.MESH
+
+    def device(slice_number, target):
+        target = (target + space) % space
+        return {
+            "x": slice_number // 2, "core": slice_number % 2, "zh": target // rest, "rest": target % rest,
+        }
+
+    crossing = core != zh
+    later, earlier = number < tm - 1, number > 0
+    barrier = pltpu.get_barrier_semaphore()
+    partner = {"core": zh, "zh": core}
+
+    def greet(where):
+        pl.semaphore_signal(barrier, inc=1, device_id=where, device_id_type=mesh_type)
+
+    @pl.when(crossing)
+    def _():
+        greet(partner)
+
+    @pl.when(later)
+    def _():
+        for shift in (-1, 0, 1):
+            greet(device(number + 1, place + shift))
+
+    @pl.when(earlier)
+    def _():
+        for shift in (-1, 0, 1):
+            greet(device(number - 1, place + shift))
+
+    amount = jnp.where(crossing, 1, 0) + jnp.where(later, 3, 0) + jnp.where(earlier, 3, 0)
+    pl.semaphore_wait(barrier, amount)
+
+    swap = pltpu.make_async_remote_copy(
+        src_ref=jump, dst_ref=landed, send_sem=swap_sems.at[0], recv_sem=swap_sems.at[1],
+        device_id=partner, device_id_type=mesh_type,
+    )
+
+    @pl.when(crossing)
+    def _():
+        swap.start()
+
+    def outgoing():
+        target = number + 1
+
+        def one(n, source, landing, shift):
+            return pltpu.make_async_remote_copy(
+                src_ref=source, dst_ref=landing, send_sem=send_sems.at[n], recv_sem=recv_sems.at[n],
+                device_id=device(target, place + shift), device_id_type=mesh_type,
+            )
+
+        return [
+            one(0, out, current.at[:, 8 : 8 + rows, :], 0),
+            one(1, edge_out.at[0], edge_in.at[1], -1),
+            one(2, edge_out.at[1], edge_in.at[0], 1),
+        ]
+
+    @pl.when(crossing)
+    def _():
+        swap.wait()
+
+    @pl.when(core == zh)
+    def _():
+        landed[...] = jump[...]
+
+    @pl.when(number == 0)
+    def _():
+        out[...] = opening[...] + landed[...]
+
+    @pl.when(earlier)
+    def _():
+        for copy in outgoing():
+            copy.wait_recv()
+        for c in range(3):
+            current[c, 7:8, :] = edge_in[0, c : c + 1, :]
+            current[c, 8 + rows : 9 + rows, :] = edge_in[1, c : c + 1, :]
+        for at in range(0, rows, 8):
+            inside = [current[c, 8 + at : 16 + at, :] for c in range(3)]
+            weights = [links[n, at : at + 8, :] for n in range(4)]
+            effective = []
+            for c in range(3):
+                m = inside[c]
+                total = weights[0] * (current[c, 7 + at : 15 + at, :] - m)
+                total = total + weights[1] * (current[c, 9 + at : 17 + at, :] - m)
+                total = total + weights[2] * (pltpu.roll(m, 1, 1) - m)
+                total = total + weights[3] * (pltpu.roll(m, grid - 1, 1) - m)
+                total = total + field[c, at : at + 8, :]
+                effective.append(total - m if c == 2 else total)
+            first = cross_of(inside, effective)
+            second = cross_of(inside, first)
+            for c in range(3):
+                value = -(first[c] + damping * second[c]) * (1.0 / (1.0 + damping * damping))
+                moved = inside[c] + FINE * step_time * value
+                out[c, at : at + 8, :] = moved + landed[c, at : at + 8, :]
+
+    @pl.when(later)
+    def _():
+        for c in range(3):
+            edge_out[0, c : c + 1, :] = out[c, 0:1, :]
+            edge_out[1, c : c + 1, :] = out[c, rows - 1 : rows, :]
+        copies = outgoing()
+        for copy in copies:
+            copy.start()
+        for copy in copies:
+            copy.wait_send()
+
+
+def sweep(space, tm, jump, opening, field, links):
+    _, rows, grid = opening.shape
+    f32 = jnp.float32
+
+    def kernel(*refs):
+        sweep_kernel(space, tm, *refs)
+
+    return pl.pallas_call(
+        kernel,
+        out_shape=jax.ShapeDtypeStruct(opening.shape, f32),
+        in_specs=[pl.BlockSpec(memory_space=pltpu.VMEM)] * 4,
+        out_specs=pl.BlockSpec(memory_space=pltpu.VMEM),
+        scratch_shapes=[
+            pltpu.VMEM((3, rows + 16, grid), f32),
+            pltpu.VMEM((3, rows, grid), f32),
+            pltpu.VMEM((2, 8, grid), f32),
+            pltpu.VMEM((2, 8, grid), f32),
+            pltpu.SemaphoreType.DMA((2,)),
+            pltpu.SemaphoreType.DMA((3,)),
+            pltpu.SemaphoreType.DMA((3,)),
+        ],
+        compiler_params=pltpu.CompilerParams(
+            collective_id=1, has_side_effects=True, vmem_limit_bytes=32 * 1024 * 1024
+        ),
+    )(jump, opening, field, links)
+
+
 def make_shards(tm, space):
     rest = space // 2
-
-    def swapped(role):
-        core, zh, r = role // space, role // rest % 2, role % rest
-        return zh * space + core * rest + r
 
     def shards(initial_state, applied_field, coupling):
         rows, _, grid = initial_state.shape
@@ -341,7 +498,6 @@
         width = length // space
         depth = tm
         part = lax.axis_index(RING)
-        old_slice = lax.axis_index(("x", "core"))
         new_slice = lax.axis_index(("x", "zh"))
         tall, blocks = real_tables(grid, space)
 
@@ -387,43 +543,21 @@
         same = ((slot >= grid)[:, None]) == ((lane >= width // 2)[None, :])
         txy = jnp.where(same, -txy, txy)
 
-        own = wide_coupling[depth : rows + depth]
-        flat = jnp.pad(own, ((0, 0), (1, 1)))
-        links = stiffness * own[None] * jnp.stack(
-            [
-                wide_coupling[depth - 1 : rows + depth - 1],
-                wide_coupling[depth + 1 : rows + depth + 1],
-                flat[:, :-2],
-                flat[:, 2:],
-            ]
-        )
+        links = links_of(wide_coupling, depth)
         cut = np.transpose(blocks.reshape(grid, space, width), (1, 0, 2))
         tables = [part_ for table in (cut, tall.T, tall, blocks.T) for part_ in halves(table)]
         jump = fine_jump(
             space, fine_start[:, depth:-depth], fine_field, links, coarse_end, jnp.stack([txx, tyy, txy, tzz]), tables
         )
-        jump = lax.ppermute(jump, LOCAL, [(swapped(i), i) for i in range(2 * space)])
-
-        def along(block, slice_shift, row_shift):
-            pairs = []
-            for device in range(tm * space):
-                n, s = device // space - slice_shift, device % space + row_shift
-                if 0 <= n and 0 <= s < space:
-                    pairs.append((n * space + s, device))
-            return lax.ppermute(block, EVERY, pairs)
-
-        def padded_from(block, slice_shift, with_middle):
-            up = along(block[:, -1:], slice_shift, -1)
-            down = along(block[:, :1], slice_shift, 1)
-            middle = along(block[:3], slice_shift, 0) if with_middle else block
-            return jnp.concatenate([up, middle, down], axis=1)
-
-        home = padded_from(jnp.concatenate([start, coupling[None]], axis=0), 0, False)
-        home_state, home_coupling = home[:3], home[3]
-        end = coarse(home_state, home_coupling, field) + jump
-        for n in range(1, tm):
-            current = jnp.where(old_slice == 0, home_state, padded_from(end, 1, True))
-            end = coarse(current, home_coupling, field) + jump
+        def beside(block, shift):
+            pairs = [(i - shift, i) for i in range(space) if 0 <= i - shift < space]
+            return lax.ppermute(block, ("zh", "rest"), pairs)
+
+        packed = jnp.concatenate([start, coupling[None]], axis=0)
+        home = jnp.concatenate([beside(packed[:, -1:], 1), packed, beside(packed[:, :1], -1)], axis=1)
+        home_coupling = home[3]
+        opening = coarse(home[:3], home_coupling, field)
+        end = sweep(space, tm, jump, opening, field, links_of(home_coupling, 1))
         return jnp.transpose(end, (1, 0, 2))[None]
 
     return shards

time: 205 us -> 176 us (0.86)
  the two profiles are of different devices: /device:TPU:18 before, /device:TPU:3 now
where the time goes in v1:
time: 176 us
  Pallas kernels  137 us (78%)
  starting transfers between devices  17.5 us (10%)
  other arithmetic  10.6 us (6%)
  waiting for transfers between devices  6.33 us (4%)
  local copies, waits for them, and re-layouts  3.52 us (2%)
    pallas_call x1, Pallas kernels, fine_jump(): pl.pallas_call(kernel, out_shape=jax.ShapeDtypeStruct(start.shape, f32),...  109 us
    pallas_call x1, Pallas kernels, sweep(): pl.pallas_call(kernel, out_shape=jax.ShapeDtypeStruct(opening.shape, f32)...  28.1 us
    ppermute x3, starting transfers between devices, fetch(): return lax.ppermute(block, LOCAL, pairs)  12.1 us
    ppermute x3, waiting for transfers between devices, fetch(): return lax.ppermute(block, LOCAL, pairs)  5.81 us
    ppermute x2, starting transfers between devices, beside(): return lax.ppermute(block, ('zh', 'rest'), pairs)  5.33 us
  transfers between devices with their start and end apart: 5, of which 2 were waited for; matrix products, arithmetic and copies ran while one was open for 2% of the time, Pallas kernels for 0%

profile of v1, /device:TPU:3, one launch (start us, length us, event | category | flops | bytes accessed | tf_op | source)
XLA Modules:
  0.0 175.6 jit_solution(11683636994242314305)
XLA Ops:
  0.0 1.3 pad_maximum_fusion.2
  1.3 4.8 %collective-permute-start.1 = (f32[7,64,512]{2,1,0:T(8,128)S(1)}, f32[7,64,512]{2,1,0:T(8,128)S(1)}, u32[]{:S(2)}, u32[]{:S(2)}) collective-permute-start(f32[7,64,512]{2,1,0:T(8,128)S(1)} %pad_maximum_fusion.2), channel_id=1, source_target_pairs={{0,0},{1,1},{2,2},{3,3},{8,4},{9,5},{10,6},{11,7},{4,8},{5,9},{6,1... | collective-permute-start | bytes 2752520 | tf_op jit(solution)/shard_map/ppermute | solution.py:515
  6.1 0.7 fusion.94
  6.8 1.3 collective-permute-start.2
  8.1 6.1 %collective-permute-start = (f32[7,4,512]{2,1,0:T(4,128)}, f32[7,4,512]{2,1,0:T(4,128)S(1)}, u32[]{:S(2)}, u32[]{:S(2)}) collective-permute-start(f32[7,4,512]{2,1,0:T(4,128)} %get-tuple-element.38), channel_id=1, source_target_pairs={{0,1},{1,2},{2,3},{8,5},{9,6},{10,7},{3,8},{4,9},{5,10},{6,11},{11... | collective-permute-start | bytes 172040 | tf_op jit(solution)/shard_map/ppermute | solution.py:515
  14.2 4.0 %collective-permute-start.4 = (f32[4,1,512]{2,1,0:T(1,128)S(1)}, f32[4,1,512]{2,1,0:T(1,128)S(1)}, u32[]{:S(2)}, u32[]{:S(2)}) collective-permute-start(f32[4,1,512]{2,1,0:T(1,128)S(1)} %get-tuple-element.43), channel_id=1, source_target_pairs={{0,1},{1,2},{2,3},{3,4},{4,5},{5,6},{6,7},{8,9},{9,10},{10,11},{11... | collective-permute-start | bytes 24584 | tf_op jit(solution)/shard_map/ppermute | solution.py:554
  18.2 1.3 collective-permute-start.3
  19.8 0.8 multiply_multiply_fusion
  20.6 1.5 pad_maximum_fusion.refs_4_
  22.1 0.5 collective-permute-done.3
  23.4 5.8 %collective-permute-done.2 = f32[7,4,512]{2,1,0:T(4,128)S(1)} collective-permute-done((f32[7,4,512]{2,1,0:T(4,128)}, f32[7,4,512]{2,1,0:T(4,128)S(1)}, u32[]{:S(2)}, u32[]{:S(2)}) %collective-permute-start.2) | collective-permute-done | bytes 57376 | tf_op jit(solution)/shard_map/ppermute | solution.py:515
  29.7 0.4 fusion.20
  30.5 0.4 fusion.28
  31.4 0.4 fusion.36
  32.0 0.4 fusion.58
  32.4 0.4 fusion.44
  33.1 0.5 fusion.61
  33.7 1.2 pad_select_fusion
  34.8 0.8 slice.464.refs_1_
  35.6 0.9 fusion.11.refs_2_
  36.5 109.2 %shard_map.109.refs_0_ = f32[3,64,512]{2,1,0:T(8,128)} custom-call(f32[3,64,512]{2,1,0:T(8,128)} %get-tuple-element.31.refs_0_, f32[3,64,512]{2,1,0:T(8,128)} %slice.464.refs_1_, f32[4,64,512]{2,1,0:T(8,128)} %fusion.11.refs_2_, f32[3,64,512]{2,1,0:T(8,128)} %get-tuple-element.30.refs_3_, f32[4,1024,128]{2,1,0:T(8,128)} %pad_maximum_fusion.refs_4_, ...), custom_call_target="tpu_custom_call" | custom-call | tf_op jit(solution)/shard_map/pallas_call | solution.py:302
  145.7 1.0 copy-done.1
  146.7 28.1 %shard_map.110 = f32[3,64,512]{2,1,0:T(8,128)S(1)} custom-call(f32[3,64,512]{2,1,0:T(8,128)S(1)} %copy-done.1, f32[3,64,512]{2,1,0:T(8,128)S(1)} %fusion.77.refs_1_, f32[3,64,512]{2,1,0:T(8,128)S(1)} %bitcast.31, f32[4,64,512]{2,1,0:T(8,128)S(1)} %maximum_multiply_fusion.refs_3_), custom_call_target="tpu_custom_call" | custom-call | tf_op jit(solution)/shard_map/pallas_call | solution.py:472
  174.9 0.7 copy.13
  (46 shorter events, 2.9 us)
Async XLA Ops:
  0.0 14.1 %copy-start.3 = (f32[64,512]{1,0:T(8,128)S(1)}, f32[64,512]{1,0:T(8,128)}, u32[]{:S(2)}) copy-start(f32[64,512]{1,0:T(8,128)} %param.13) | copy-start | bytes 393220
  0.0 14.1 %copy-start.2 = (f32[64,3,512]{2,0,1:T(8,128)S(1)}, f32[64,3,512]{2,0,1:T(8,128)}, u32[]{:S(2)}) copy-start(f32[64,3,512]{2,0,1:T(8,128)} %param.11) | copy-start | bytes 1179652
  1.3 27.9 %collective-permute-start.1 = (f32[7,64,512]{2,1,0:T(8,128)S(1)}, f32[7,64,512]{2,1,0:T(8,128)S(1)}, u32[]{:S(2)}, u32[]{:S(2)}) collective-permute-start(f32[7,64,512]{2,1,0:T(8,128)S(1)} %pad_maximum_fusion.2), channel_id=1, source_target_pairs={{0,0},{1,1},{2,2},{3,3},{8,4},{9,5},{10,6},{11,7},{4,8},{5,9},{6,1... | collective-permute-start | bytes 2752520 | tf_op jit(solution)/shard_map/ppermute | solution.py:515
  6.8 22.4 %collective-permute-start.2 = (f32[7,4,512]{2,1,0:T(4,128)}, f32[7,4,512]{2,1,0:T(4,128)S(1)}, u32[]{:S(2)}, u32[]{:S(2)}) collective-permute-start(f32[7,4,512]{2,1,0:T(4,128)} %get-tuple-element.39), channel_id=1, source_target_pairs={{1,0},{2,1},{3,2},{4,3},{9,4},{10,5},{11,6},{12,7},{5,8},{6,9},{7,... | collective-permute-start | bytes 172040 | tf_op jit(solution)/shard_map/ppermute | solution.py:515
  8.1 21.1 %collective-permute-start = (f32[7,4,512]{2,1,0:T(4,128)}, f32[7,4,512]{2,1,0:T(4,128)S(1)}, u32[]{:S(2)}, u32[]{:S(2)}) collective-permute-start(f32[7,4,512]{2,1,0:T(4,128)} %get-tuple-element.38), channel_id=1, source_target_pairs={{0,1},{1,2},{2,3},{8,5},{9,6},{10,7},{3,8},{4,9},{5,10},{6,11},{11... | collective-permute-start | bytes 172040 | tf_op jit(solution)/shard_map/ppermute | solution.py:515
  14.2 7.9 %collective-permute-start.4 = (f32[4,1,512]{2,1,0:T(1,128)S(1)}, f32[4,1,512]{2,1,0:T(1,128)S(1)}, u32[]{:S(2)}, u32[]{:S(2)}) collective-permute-start(f32[4,1,512]{2,1,0:T(1,128)S(1)} %get-tuple-element.43), channel_id=1, source_target_pairs={{0,1},{1,2},{2,3},{3,4},{4,5},{5,6},{6,7},{8,9},{9,10},{10,11},{11... | collective-permute-start | bytes 24584 | tf_op jit(solution)/shard_map/ppermute | solution.py:554
  18.2 4.4 %collective-permute-start.3 = (f32[4,1,512]{2,1,0:T(1,128)S(1)}, f32[4,1,512]{2,1,0:T(1,128)S(1)}, u32[]{:S(2)}, u32[]{:S(2)}) collective-permute-start(f32[4,1,512]{2,1,0:T(1,128)S(1)} %get-tuple-element.42), channel_id=1, source_target_pairs={{1,0},{2,1},{3,2},{4,3},{5,4},{6,5},{7,6},{9,8},{10,9},{11,10},{12... | collective-permute-start | bytes 24584 | tf_op jit(solution)/shard_map/ppermute | solution.py:554
  20.6 2.1 %copy-start = (f32[64,3,512]{2,0,1:T(8,128)S(1)}, f32[64,3,512]{2,0,1:T(8,128)}, u32[]{:S(2)}) copy-start(f32[64,3,512]{2,0,1:T(8,128)} %param.12) | copy-start | bytes 1179652
  145.7 1.0 copy-start.1
